TPU v7x, 512 devices: a whole 4x8x8 slice. The times are simulated.
512 devices in a mesh: row: 32 (over z, x_hi, core), col: 16 (over y, x_lo).
Axes of the slice: x: 4 (x_hi: 2, x_lo: 2; x = x_hi * 2 + x_lo), y: 8, z: 8, core: 2. Of those that a mesh axis runs over, the one named last changes fastest.
Arguments:
- ancestor: float32 [32, 384, 12288], P(None, 'col', 'row'), may hold values from -6 to 6
- panels: float32 [2, 12288, 512], P(None, ('row', 'col')), may hold values from -0.06 to 0.06
- link_panels: float32 [1, 512, 512], P(None, 'row'), may hold values from -0.25 to 0.25
- diag_inverse: float32 [2, 512, 512], P(None, 'row'), may hold values from -0.25 to 0.25
- blocks: int32 [2, 48], replicated, may hold values from 0 to 95, as said below
Outputs:
- columns: float32 [2, 12288, 512], P(None, ('row', 'col'))
- diagonal: float32 [2, 512, 512], P(None, 'row', 'col')
Inputs may be any that keep to these rules, and one draw needn't show every extreme that they name: Each of the 2 rows names 48 different row blocks.
All inputs are finite; a program needn't handle non-finite values.
Results may differ from a plain program's by a relative error of at most 0.0001.
Values sent between devices are 32-bit elements; how exact they have to be, the bound alone decides.
A program may use at most 64 MiB of HBM per device.

v0:
```python
import jax
import jax.numpy as jnp
from jax import lax
from jax.sharding import Mesh
from jax.sharding import PartitionSpec as P

BLOCK = 128
ROW = ("row_0", "row_1", "row_2")
ROW_COL = ("row_0", "row_1", "row_2", "col")


def joined_along(blocks, dim):
    blocks = jnp.moveaxis(blocks, 0, dim)
    shape = blocks.shape
    return blocks.reshape(*shape[:dim], shape[dim] * shape[dim + 1], *shape[dim + 2 :])


def gather_in_order(shard, axes, turns):
    blocks = shard[None]
    for k in turns:
        blocks = lax.all_gather(blocks, axes[k], axis=0, tiled=True)
    block = [lax.axis_size(axes[k]) for k in reversed(turns)]
    blocks = blocks.reshape(*block, *shard.shape)
    turned = sorted(range(len(turns)), key=lambda place: turns[len(turns) - 1 - place])
    return blocks.transpose(*turned, *range(len(turns), blocks.ndim)).reshape(-1, *shard.shape)


def gather_axes(shard, axes, turns, dim):
    return joined_along(gather_in_order(shard, axes, turns), dim)


def split_up(shard, dim, length):
    before, after = (shard.shape[:dim], shard.shape[dim + 1 :])
    return jnp.moveaxis(shard.reshape(*before, length, -1, *after), dim, 0)


def sum_at_owner(shard, axis, dim):
    blocks = split_up(shard, dim, lax.axis_size(axis))
    arrived = lax.all_to_all(blocks, axis, split_axis=0, concat_axis=0, tiled=True)
    return arrived.sum(axis=0)


def from_everyone(shard, axis):
    length = lax.axis_size(axis)
    return lax.all_to_all(
        jnp.broadcast_to(shard[None], (length, *shard.shape)), axis, 0, 0, tiled=True
    )


def collect(shard, axis, dim):
    return joined_along(from_everyone(shard, axis), dim)


def matmul(left, right):
    return jnp.dot(left, right, precision=lax.Precision.HIGHEST, preferred_element_type=jnp.float32)


def matmul_left_t(left, right):
    return lax.dot_general(
        left,
        right,
        (((0,), (0,)), ((), ())),
        precision=lax.Precision.HIGHEST,
        preferred_element_type=jnp.float32,
    )


def select_rows(values, row_block, chosen):
    hit = jnp.any(row_block[:, None] == chosen[None, :], axis=1)
    return jnp.where(hit[:, None], values, jnp.float32(0.0))


def body(ancestor, panels, link_panels, diag_inverse, blocks):
    row_count = lax.axis_size(ROW)
    col_count = lax.axis_size("col")
    row_index = lax.axis_index(ROW)
    col_index = lax.axis_index("col")
    resident_t = ancestor.reshape(ancestor.shape[0] * ancestor.shape[1], ancestor.shape[2])
    supernodes = panels.shape[0]
    rows_here = panels.shape[1]
    panel_width = panels.shape[2]
    rows_part = panel_width // row_count
    cols_part = panel_width // col_count
    first_row = (row_index * col_count + col_index) * rows_here
    row_block = (first_row + jnp.arange(rows_here, dtype=jnp.int32)) // BLOCK
    masked = jnp.stack(
        [select_rows(panels[number], row_block, blocks[number]) for number in range(supernodes)]
    )
    joined = jnp.transpose(masked, (1, 0, 2)).reshape(rows_here, supernodes * panel_width)
    folded = matmul_left_t(resident_t, gather_axes(joined, ROW, (1, 0, 2), 0))
    summed = sum_at_owner(folded, "col", 0).reshape(rows_here, supernodes, panel_width)
    links_all = lax.all_gather(link_panels, ROW, axis=1, tiled=True)
    global_rows = row_index * rows_part + jnp.arange(rows_part, dtype=jnp.int32)
    lower_keep = jnp.arange(panel_width, dtype=jnp.int32)[None, :] <= global_rows[:, None]
    col_list = []
    diag_list = []
    prev_cols = None
    prev_rows = None
    for supernode in range(supernodes):
        local_panel = masked[supernode]
        product = summed[:, supernode, :]
        if supernode > 0:
            link = links_all[supernode - 1]
        lowered = jnp.where(lower_keep, diag_inverse[supernode], jnp.float32(0.0))
        right_part = lax.dynamic_slice_in_dim(lowered, col_index * cols_part, cols_part, 1)
        share = matmul(lowered.T, right_part)
        if supernode == 0:
            cols_now = -product
            partial_value = -matmul(local_panel.T, cols_now)
        else:
            carried = matmul(prev_cols, link)
            cols_now = -(product + carried)
            partial_value = matmul(carried.T, local_panel) - matmul(local_panel.T, cols_now)
            link_cols = lax.dynamic_slice_in_dim(link, col_index * cols_part, cols_part, 1)
            link_rows = lax.dynamic_slice_in_dim(link, row_index * rows_part, rows_part, 0)
            share = share + matmul(link_rows.T, matmul(prev_rows, link_cols))
        current = lax.dynamic_slice_in_dim(partial_value, col_index * cols_part, cols_part, 1)
        partial_value = lax.dynamic_update_slice_in_dim(
            partial_value, current + share, col_index * cols_part, 1
        )
        column_block = sum_at_owner(partial_value, "col", 1)
        diag_block = sum_at_owner(column_block, ROW, 0)
        if supernode + 1 < supernodes:
            prev_rows = collect(diag_block, "col", 1)
        col_list.append(cols_now)
        diag_list.append(diag_block)
        prev_cols = cols_now
    return (jnp.stack(col_list), jnp.stack(diag_list))


def solution(mesh):
    torus = Mesh(
        mesh.devices.reshape(8, 2, 2, mesh.shape["col"]), ("row_0", "row_1", "row_2", "col")
    )
    return jax.shard_map(
        body,
        mesh=torus,
        in_specs=(
            P(None, "col", ROW),
            P(None, ROW_COL, None),
            P(None, ROW, None),
            P(None, ROW, None),
            P(),
        ),
        out_specs=(P(None, ROW_COL, None), P(None, ROW, "col")),
        check_vma=False,
    )
```

profile of v0, /device:TPU:1, one launch (start us, length us, event | category | flops | bytes accessed | tf_op | source)
XLA Modules:
  0.0 295.9 jit_solution(991701370696724680)
XLA Ops:
  8.1 0.8 slice_bitcast_fusion
  9.1 0.9 slice_select_fusion
  10.1 6.3 %all_gather.12 = f32[2,24,1024]{2,1,0:T(8,128)} all-gather(f32[1,24,1024]{2,1,0:T(8,128)S(1)} %broadcast_in_dim_reshape.3), channel_id=1, replica_groups=mesh['row_0'=8,'row_1'=2,'row_2'=2,'col'=16] {'row_1'}, dimensions={0}, use_global_device_ids=true | all-gather | bytes 294912 | tf_op jit(solution)/shard_map/all_gather | solution.py:21
  16.5 45.2 %all-gather.4.cloned.1.call-done = f32[16,24,1024]{2,1,0:T(8,128)} async-done(((f32[2,24,1024]{2,1,0:T(8,128)}), f32[16,24,1024]{2,1,0:T(8,128)}) %all-gather.4.cloned.1.call-update) | async-done | bytes 1572880 | tf_op jit(solution)/shard_map/all_gather | solution.py:21
  61.7 25.8 %all-gather.6.cloned.1.call-done = f32[32,24,1024]{2,1,0:T(8,128)} async-done(((f32[16,24,1024]{2,1,0:T(8,128)}), f32[32,24,1024]{2,1,0:T(8,128)}) %all-gather.6.cloned.1.call-update) | async-done | bytes 3145744 | tf_op jit(solution)/shard_map/all_gather | solution.py:21
  87.6 2.1 copy.23
  89.7 5.2 %fusion.35 = f32[1024,384]{0,1:T(8,128)} fusion(f32[768,1024]{1,0:T(8,128)S(1)} %bitcast.71, f32[768,384]{1,0:T(8,128)S(1)} %bitcast.70), kind=kOutput, calls=%fused_computation.58 | convolution fusion | flops 3623878656 | bytes 5898240 | tf_op jit(solution)/shard_map/dot_general | solution.py:59
  94.9 6.6 %all-to-all-start = ((f32[16,24,1024]{2,1,0:T(8,128)}), f32[16,24,1024]{2,1,0:T(8,128)S(1)}, u32[]{:S(2)}, u32[]{:S(2)}) async-start(f32[16,24,1024]{2,1,0:T(8,128)} %bitcast.72), calls=%async_computation | async-start | bytes 3145728 | tf_op jit(solution)/shard_map/all_to_all | solution.py:39
  102.2 35.6 %all-to-all-done = f32[16,24,1024]{2,1,0:T(8,128)S(1)} async-done(((f32[16,24,1024]{2,1,0:T(8,128)}), f32[16,24,1024]{2,1,0:T(8,128)S(1)}, u32[]{:S(2)}, u32[]{:S(2)}) %all-to-all-start) | async-done | bytes 1572896 | tf_op jit(solution)/shard_map/all_to_all | solution.py:39
  138.0 2.0 convolution_negate_fusion
  140.0 1.8 fusion.2
  141.8 6.6 %all-to-all-start.1 = ((f32[16,512,32]{1,2,0:T(8,128)}), f32[16,512,32]{1,2,0:T(8,128)S(1)}, u32[]{:S(2)}, u32[]{:S(2)}) async-start(f32[16,512,32]{1,2,0:T(8,128)} %bitcast.17), calls=%async_computation.1 | async-start | bytes 2097152 | tf_op jit(solution)/shard_map/all_to_all | solution.py:39
  148.8 50.5 %all-gather.8.cloned.1.call-done = f32[1,512,512]{2,1,0:T(8,128)} async-done(((f32[1,16,512]{2,1,0:T(8,128)}), f32[1,512,512]{2,1,0:T(8,128)}) %all-gather.8.cloned.1.call-update) | async-done | bytes 1048592 | tf_op jit(solution)/shard_map/all_gather | solution.py:92
  199.3 1.8 fusion.3
  201.4 0.8 reshape.96
  202.2 4.9 %all-to-all-start.2 = ((f32[32,1,512]{2,1,0:T(1,128)}), f32[32,1,512]{2,1,0:T(1,128)S(1)}, u32[]{:S(2)}, u32[]{:S(2)}) async-start(f32[32,1,512]{2,1,0:T(1,128)} %reshape.96), calls=%async_computation.2 | async-start | bytes 131072 | tf_op jit(solution)/shard_map/all_to_all | solution.py:39
  207.1 1.1 fusion.13
  208.2 8.7 %all-to-all-done.2 = f32[32,1,512]{2,1,0:T(1,128)S(1)} async-done(((f32[32,1,512]{2,1,0:T(1,128)}), f32[32,1,512]{2,1,0:T(1,128)S(1)}, u32[]{:S(2)}, u32[]{:S(2)}) %all-to-all-start.2) | async-done | bytes 65568 | tf_op jit(solution)/shard_map/all_to_all | solution.py:39
  217.4 0.8 reduce
  218.4 0.7 reshape.98
  219.1 8.2 %all-to-all-start.3 = ((f32[16,1,512]{2,1,0:T(1,128)}), f32[16,1,512]{2,1,0:T(1,128)S(1)}, u32[]{:S(2)}, u32[]{:S(2)}) async-start(f32[16,1,512]{2,1,0:T(1,128)} %reshape.98), calls=%async_computation.3 | async-start | bytes 65536 | tf_op jit(solution)/shard_map/all_to_all | solution.py:45
  227.3 2.0 convolution_subtract_fusion
  229.3 5.7 %all-to-all-done.3 = f32[16,1,512]{2,1,0:T(1,128)S(1)} async-done(((f32[16,1,512]{2,1,0:T(1,128)}), f32[16,1,512]{2,1,0:T(1,128)S(1)}, u32[]{:S(2)}, u32[]{:S(2)}) %all-to-all-start.3) | async-done | bytes 32800 | tf_op jit(solution)/shard_map/all_to_all | solution.py:45
  235.0 0.7 reduce.1
  236.0 1.3 fusion.5
  237.3 1.7 fusion.1
  239.0 3.7 %all-to-all-start.4 = ((f32[16,512,32]{1,2,0:T(8,128)}), f32[16,512,32]{1,2,0:T(8,128)S(1)}, u32[]{:S(2)}, u32[]{:S(2)}) async-start(f32[16,512,32]{1,2,0:T(8,128)} %bitcast.26), calls=%async_computation.4 | async-start | bytes 2097152 | tf_op jit(solution)/shard_map/all_to_all | solution.py:39
  242.7 24.4 %all-to-all-done.4 = f32[16,512,32]{1,2,0:T(8,128)S(1)} async-done(((f32[16,512,32]{1,2,0:T(8,128)}), f32[16,512,32]{1,2,0:T(8,128)S(1)}, u32[]{:S(2)}, u32[]{:S(2)}) %all-to-all-start.4) | async-done | bytes 1048608 | tf_op jit(solution)/shard_map/all_to_all | solution.py:39
  267.3 0.8 reshape.100
  268.1 8.8 %all-to-all-start.5 = ((f32[32,1,512]{2,1,0:T(1,128)}), f32[32,1,512]{2,1,0:T(1,128)S(1)}, u32[]{:S(2)}, u32[]{:S(2)}) async-start(f32[32,1,512]{2,1,0:T(1,128)} %reshape.100), calls=%async_computation.5 | async-start | bytes 131072 | tf_op jit(solution)/shard_map/all_to_all | solution.py:39
  277.6 9.2 %all-to-all-done.5 = f32[32,1,512]{2,1,0:T(1,128)S(1)} async-done(((f32[32,1,512]{2,1,0:T(1,128)}), f32[32,1,512]{2,1,0:T(1,128)S(1)}, u32[]{:S(2)}, u32[]{:S(2)}) %all-to-all-start.5) | async-done | bytes 65568 | tf_op jit(solution)/shard_map/all_to_all | solution.py:39
  286.8 0.8 reduce.2
  (41 shorter events, 4.5 us)
Async XLA Ops:
  8.0 81.7 %copy-start = (f32[32,24,384]{2,1,0:T(8,128)S(1)}, f32[32,24,384]{2,1,0:T(8,128)}, u32[]{:S(2)}) copy-start(f32[32,24,384]{2,1,0:T(8,128)} %param.5) | copy-start | bytes 3538948
  8.0 53.7 %all-gather.4.cloned.1.call-start = ((), (), s32[]{:S(2)}) async-start(), calls=%async_computation.6 | async-start | bytes 1769472 | tf_op jit(solution)/shard_map/all_gather | solution.py:21
  16.5 71.1 %all-gather.6.cloned.1.call-start = ((), (), s32[]{:S(2)}) async-start(), calls=%async_computation.7 | async-start | bytes 4718592 | tf_op jit(solution)/shard_map/all_gather | solution.py:21
  94.9 7.2 %copy-start.2 = (f32[2,16,512]{2,1,0:T(8,128)S(1)}, f32[2,16,512]{2,1,0:T(8,128)}, u32[]{:S(2)}) copy-start(f32[2,16,512]{2,1,0:T(8,128)} %param.8) | copy-start | bytes 196612
  94.9 42.9 %all-to-all-start = ((f32[16,24,1024]{2,1,0:T(8,128)}), f32[16,24,1024]{2,1,0:T(8,128)S(1)}, u32[]{:S(2)}, u32[]{:S(2)}) async-start(f32[16,24,1024]{2,1,0:T(8,128)} %bitcast.72), calls=%async_computation | async-start | bytes 3145728 | tf_op jit(solution)/shard_map/all_to_all | solution.py:39
  101.5 97.8 %all-gather.8.cloned.1.call-start = ((), (), s32[]{:S(2)}) async-start(), calls=%async_computation.8 | async-start | bytes 1081344 | tf_op jit(solution)/shard_map/all_gather | solution.py:92
  141.8 59.4 %all-to-all-start.1 = ((f32[16,512,32]{1,2,0:T(8,128)}), f32[16,512,32]{1,2,0:T(8,128)S(1)}, u32[]{:S(2)}, u32[]{:S(2)}) async-start(f32[16,512,32]{1,2,0:T(8,128)} %bitcast.17), calls=%async_computation.1 | async-start | bytes 2097152 | tf_op jit(solution)/shard_map/all_to_all | solution.py:39
  148.5 58.6 %copy-start.1 = (f32[2,24,512]{2,1,0:T(8,128)S(1)}, f32[2,24,512]{2,1,0:T(8,128)}, u32[]{:S(2)}) copy-start(f32[2,24,512]{2,1,0:T(8,128)} %param.6) | copy-start | bytes 294916
  202.2 14.7 %all-to-all-start.2 = ((f32[32,1,512]{2,1,0:T(1,128)}), f32[32,1,512]{2,1,0:T(1,128)S(1)}, u32[]{:S(2)}, u32[]{:S(2)}) async-start(f32[32,1,512]{2,1,0:T(1,128)} %reshape.96), calls=%async_computation.2 | async-start | bytes 131072 | tf_op jit(solution)/shard_map/all_to_all | solution.py:39
  219.1 15.9 %all-to-all-start.3 = ((f32[16,1,512]{2,1,0:T(1,128)}), f32[16,1,512]{2,1,0:T(1,128)S(1)}, u32[]{:S(2)}, u32[]{:S(2)}) async-start(f32[16,1,512]{2,1,0:T(1,128)} %reshape.98), calls=%async_computation.3 | async-start | bytes 65536 | tf_op jit(solution)/shard_map/all_to_all | solution.py:45
  239.0 28.1 %all-to-all-start.4 = ((f32[16,512,32]{1,2,0:T(8,128)}), f32[16,512,32]{1,2,0:T(8,128)S(1)}, u32[]{:S(2)}, u32[]{:S(2)}) async-start(f32[16,512,32]{1,2,0:T(8,128)} %bitcast.26), calls=%async_computation.4 | async-start | bytes 2097152 | tf_op jit(solution)/shard_map/all_to_all | solution.py:39
  268.1 18.7 %all-to-all-start.5 = ((f32[32,1,512]{2,1,0:T(1,128)}), f32[32,1,512]{2,1,0:T(1,128)S(1)}, u32[]{:S(2)}, u32[]{:S(2)}) async-start(f32[32,1,512]{2,1,0:T(1,128)} %reshape.100), calls=%async_computation.5 | async-start | bytes 131072 | tf_op jit(solution)/shard_map/all_to_all | solution.py:39
Sparse Core Ops, SparseCore 0:
  16.6 45.0 all-gather.3
  63.8 23.6 all-gather.5
Sparse Core Ops, SparseCore 1:
  105.3 93.9 all-gather.7
where the time goes:
time: 297 us; the launch traced here: 296 us
  waiting for transfers between devices  206 us (69%)
  starting transfers between devices  38.9 us (13%)
  matrix products  17.3 us (6%)
  between operations  15.8 us (5%)
  local copies, waits for them, and re-layouts  6.79 us (2%)
  blocking collectives  6.33 us (2%)
  other arithmetic  5.08 us (2%)
    all_to_all x5, waiting for transfers between devices, sum_at_owner(): lax.all_to_all(blocks, axis, split_axis=0, concat_axis=0, tiled=True)  77.9 us
    all_gather x2, waiting for transfers between devices, gather_in_order(): blocks = lax.all_gather(blocks, axes[k], axis=0, tiled=True)  71 us
    all_gather x1, waiting for transfers between devices, body(): links_all = lax.all_gather(link_panels, ROW, axis=1, tiled=True)  50.5 us
    all_to_all x5, starting transfers between devices, sum_at_owner(): lax.all_to_all(blocks, axis, split_axis=0, concat_axis=0, tiled=True)  30.6 us
    dot_general x8, matrix products, matmul(): jnp.dot(left, right, precision=lax.Precision.HIGHEST, preferred_element_t...  12.1 us
    all_to_all x1, starting transfers between devices, from_everyone(): lax.all_to_all(jnp.broadcast_to(shard[None], (length, *shard.shape)), axi...  8.19 us
    all_gather x1, blocking collectives, gather_in_order(): blocks = lax.all_gather(blocks, axes[k], axis=0, tiled=True)  6.33 us
  transfers between devices with their start and end apart: 9, of which 8 were waited for; matrix products, arithmetic and copies ran while one was open for 3% of the time, Pallas kernels for 0%

commit v1 on v0

--- a/solution.py
+++ b/solution.py
@@ -18,7 +18,16 @@
 def gather_in_order(shard, axes, turns):
     blocks = shard[None]
     for k in turns:
-        blocks = lax.all_gather(blocks, axes[k], axis=0, tiled=True)
+        pack_the_knots = lambda s0, mesh_dim: jnp.concatenate(
+            jax.lax.all_to_all(
+                jnp.stack([s0 for _ in range(jax.lax.axis_size(mesh_dim))]),
+                mesh_dim,
+                split_axis=0,
+                concat_axis=0,
+            ),
+            0,
+        )
+        blocks = pack_the_knots(blocks, axes[k])
     block = [lax.axis_size(axes[k]) for k in reversed(turns)]
     blocks = blocks.reshape(*block, *shard.shape)
     turned = sorted(range(len(turns)), key=lambda place: turns[len(turns) - 1 - place])

time: 297 us -> 278 us (0.936)
  waiting for transfers between devices: 206 us -> 127 us
  blocking collectives: 6.33 us -> 66.4 us
    all_gather x2 -> x0, waiting for transfers between devices: 71 us -> none  [gather_in_order(): blocks = lax.all_gather(blocks, axes[k], axis=0, tiled=True)]
    all_to_all x0 -> x3, blocking collectives: none -> 66.4 us  [gather_in_order(): jax.lax.all_to_all(jnp.stack([s0 for _ in range(jax.lax.axis_size(mesh_di...]
    all_gather x1, waiting for transfers between devices: 50.5 us -> 43.7 us  [body(): links_all = lax.all_gather(link_panels, ROW, axis=1, tiled=True)]
    all_gather x1 -> x0, blocking collectives: 6.33 us -> none  [gather_in_order(): blocks = lax.all_gather(blocks, axes[k], axis=0, tiled=True)]
  transfers between devices with their start and end apart: 9 -> 7, of which waited for: 8 -> 6; matrix products, arithmetic and copies ran while one was open for 3% -> 4% of each run, Pallas kernels for 0% -> 0%
where the time goes in v1:
time: 278 us; the launch traced here: 277 us
  waiting for transfers between devices  127 us (46%)
  blocking collectives  66.4 us (24%)
  starting transfers between devices  40.6 us (15%)
  matrix products  17.3 us (6%)
  between operations  14.3 us (5%)
  other arithmetic  5.5 us (2%)
  local copies, waits for them, and re-layouts  5.27 us (2%)
    all_to_all x5, waiting for transfers between devices, sum_at_owner(): lax.all_to_all(blocks, axis, split_axis=0, concat_axis=0, tiled=True)  77.4 us
    all_to_all x3, blocking collectives, gather_in_order(): jax.lax.all_to_all(jnp.stack([s0 for _ in range(jax.lax.axis_size(mesh_di...  66.4 us
    all_gather x1, waiting for transfers between devices, body(): links_all = lax.all_gather(link_panels, ROW, axis=1, tiled=True)  43.7 us
    all_to_all x5, starting transfers between devices, sum_at_owner(): lax.all_to_all(blocks, axis, split_axis=0, concat_axis=0, tiled=True)  32.4 us
    dot_general x8, matrix products, matmul(): jnp.dot(left, right, precision=lax.Precision.HIGHEST, preferred_element_t...  12.1 us
    all_to_all x1, starting transfers between devices, from_everyone(): lax.all_to_all(jnp.broadcast_to(shard[None], (length, *shard.shape)), axi...  8.1 us
    all_to_all x1, waiting for transfers between devices, from_everyone(): lax.all_to_all(jnp.broadcast_to(shard[None], (length, *shard.shape)), axi...  5.68 us
  transfers between devices with their start and end apart: 7, of which 6 were waited for; matrix products, arithmetic and copies ran while one was open for 4% of the time, Pallas kernels for 0%

profile of v1, /device:TPU:1, one launch (start us, length us, event | category | flops | bytes accessed | tf_op | source)
XLA Modules:
  0.0 276.9 jit_solution(16548071423429158233)
XLA Ops:
  7.2 0.8 slice_bitcast_fusion
  8.2 0.9 slice_select_fusion
  9.3 9.8 %all_to_all.45 = f32[2,1,24,1024]{3,2,1,0:T(8,128)S(1)} all-to-all(f32[2,1,24,1024]{3,2,1,0:T(8,128)S(1)} %pad_maximum_fusion.1), channel_id=1, replica_groups=mesh['row_0'=8,'row_1'=2,'row_2'=2,'col'=16] {'row_1'}, dimensions={0} | all-to-all | bytes 393216 | tf_op jit(solution)/shard_map/all_to_all | solution.py:22
  19.3 46.8 %all_to_all.46 = f32[8,2,24,1024]{3,2,1,0:T(8,128)S(1)} all-to-all(f32[8,2,24,1024]{3,2,1,0:T(8,128)S(1)} %stack.32), channel_id=1, replica_groups=mesh['row_0'=8,'row_1'=2,'row_2'=2,'col'=16] {'row_0'}, dimensions={0} | all-to-all | bytes 3145728 | tf_op jit(solution)/shard_map/all_to_all | solution.py:22
  66.5 9.8 %all_to_all.47 = f32[2,16,24,1024]{3,2,1,0:T(8,128)S(1)} all-to-all(f32[2,16,24,1024]{3,2,1,0:T(8,128)S(1)} %pad_maximum_fusion), channel_id=1, replica_groups=mesh['row_0'=8,'row_1'=2,'row_2'=2,'col'=16] {'row_2'}, dimensions={0} | all-to-all | bytes 6291456 | tf_op jit(solution)/shard_map/all_to_all | solution.py:22
  76.8 5.2 %fusion.35 = f32[1024,384]{0,1:T(8,128)} fusion(f32[768,1024]{1,0:T(8,128)S(1)} %bitcast.74, f32[768,384]{1,0:T(8,128)S(1)} %bitcast.73), kind=kOutput, calls=%fused_computation.60 | convolution fusion | flops 3623878656 | bytes 5898240 | tf_op jit(solution)/shard_map/dot_general | solution.py:68
  82.0 7.1 %all-to-all-start.3 = ((f32[16,24,1024]{2,1,0:T(8,128)}), f32[16,24,1024]{2,1,0:T(8,128)S(1)}, u32[]{:S(2)}, u32[]{:S(2)}) async-start(f32[16,24,1024]{2,1,0:T(8,128)} %bitcast.75), calls=%async_computation.3 | async-start | bytes 3145728 | tf_op jit(solution)/shard_map/all_to_all | solution.py:48
  89.1 0.7 all-gather.2.cloned.1.call-update
  89.9 35.0 %all-to-all-done.3 = f32[16,24,1024]{2,1,0:T(8,128)S(1)} async-done(((f32[16,24,1024]{2,1,0:T(8,128)}), f32[16,24,1024]{2,1,0:T(8,128)S(1)}, u32[]{:S(2)}, u32[]{:S(2)}) %all-to-all-start.3) | async-done | bytes 1572896 | tf_op jit(solution)/shard_map/all_to_all | solution.py:48
  125.2 2.0 convolution_negate_fusion
  127.2 1.8 fusion.2
  129.0 7.1 %all-to-all-start.4 = ((f32[16,512,32]{1,2,0:T(8,128)}), f32[16,512,32]{1,2,0:T(8,128)S(1)}, u32[]{:S(2)}, u32[]{:S(2)}) async-start(f32[16,512,32]{1,2,0:T(8,128)} %bitcast.19), calls=%async_computation.4 | async-start | bytes 2097152 | tf_op jit(solution)/shard_map/all_to_all | solution.py:48
  136.5 43.7 %all-gather.2.cloned.1.call-done = f32[1,512,512]{2,1,0:T(8,128)} async-done(((f32[1,16,512]{2,1,0:T(8,128)}), f32[1,512,512]{2,1,0:T(8,128)}) %all-gather.2.cloned.1.call-update) | async-done | bytes 1048592 | tf_op jit(solution)/shard_map/all_gather | solution.py:101
  180.1 1.8 fusion.3
  182.2 0.8 reshape.94
  183.0 5.8 %all-to-all-start.5 = ((f32[32,1,512]{2,1,0:T(1,128)}), f32[32,1,512]{2,1,0:T(1,128)S(1)}, u32[]{:S(2)}, u32[]{:S(2)}) async-start(f32[32,1,512]{2,1,0:T(1,128)} %reshape.94), calls=%async_computation.5 | async-start | bytes 131072 | tf_op jit(solution)/shard_map/all_to_all | solution.py:48
  188.8 1.1 fusion.13
  189.9 8.7 %all-to-all-done.5 = f32[32,1,512]{2,1,0:T(1,128)S(1)} async-done(((f32[32,1,512]{2,1,0:T(1,128)}), f32[32,1,512]{2,1,0:T(1,128)S(1)}, u32[]{:S(2)}, u32[]{:S(2)}) %all-to-all-start.5) | async-done | bytes 65568 | tf_op jit(solution)/shard_map/all_to_all | solution.py:48
  199.1 0.8 reduce
  200.1 0.7 reshape.96
  200.8 8.1 %all-to-all-start.6 = ((f32[16,1,512]{2,1,0:T(1,128)}), f32[16,1,512]{2,1,0:T(1,128)S(1)}, u32[]{:S(2)}, u32[]{:S(2)}) async-start(f32[16,1,512]{2,1,0:T(1,128)} %reshape.96), calls=%async_computation.6 | async-start | bytes 65536 | tf_op jit(solution)/shard_map/all_to_all | solution.py:54
  208.9 2.0 convolution_subtract_fusion
  211.0 5.7 %all-to-all-done.6 = f32[16,1,512]{2,1,0:T(1,128)S(1)} async-done(((f32[16,1,512]{2,1,0:T(1,128)}), f32[16,1,512]{2,1,0:T(1,128)S(1)}, u32[]{:S(2)}, u32[]{:S(2)}) %all-to-all-start.6) | async-done | bytes 32800 | tf_op jit(solution)/shard_map/all_to_all | solution.py:54
  216.6 0.7 reduce.1
  217.6 1.3 fusion.5
  218.9 1.7 fusion.1
  220.6 3.7 %all-to-all-start.7 = ((f32[16,512,32]{1,2,0:T(8,128)}), f32[16,512,32]{1,2,0:T(8,128)S(1)}, u32[]{:S(2)}, u32[]{:S(2)}) async-start(f32[16,512,32]{1,2,0:T(8,128)} %bitcast.28), calls=%async_computation.7 | async-start | bytes 2097152 | tf_op jit(solution)/shard_map/all_to_all | solution.py:48
  224.3 24.4 %all-to-all-done.7 = f32[16,512,32]{1,2,0:T(8,128)S(1)} async-done(((f32[16,512,32]{1,2,0:T(8,128)}), f32[16,512,32]{1,2,0:T(8,128)S(1)}, u32[]{:S(2)}, u32[]{:S(2)}) %all-to-all-start.7) | async-done | bytes 1048608 | tf_op jit(solution)/shard_map/all_to_all | solution.py:48
  248.9 0.8 reshape.98
  249.7 8.8 %all-to-all-start.8 = ((f32[32,1,512]{2,1,0:T(1,128)}), f32[32,1,512]{2,1,0:T(1,128)S(1)}, u32[]{:S(2)}, u32[]{:S(2)}) async-start(f32[32,1,512]{2,1,0:T(1,128)} %reshape.98), calls=%async_computation.8 | async-start | bytes 131072 | tf_op jit(solution)/shard_map/all_to_all | solution.py:48
  259.2 9.2 %all-to-all-done.8 = f32[32,1,512]{2,1,0:T(1,128)S(1)} async-done(((f32[32,1,512]{2,1,0:T(1,128)}), f32[32,1,512]{2,1,0:T(1,128)S(1)}, u32[]{:S(2)}, u32[]{:S(2)}) %all-to-all-start.8) | async-done | bytes 65568 | tf_op jit(solution)/shard_map/all_to_all | solution.py:48
  268.4 0.8 reduce.2
  (40 shorter events, 4.8 us)
Async XLA Ops:
  7.2 69.6 %copy-start = (f32[32,24,384]{2,1,0:T(8,128)S(1)}, f32[32,24,384]{2,1,0:T(8,128)}, u32[]{:S(2)}) copy-start(f32[32,24,384]{2,1,0:T(8,128)} %param.5) | copy-start | bytes 3538948
  82.0 7.9 %copy-start.2 = (f32[2,16,512]{2,1,0:T(8,128)S(1)}, f32[2,16,512]{2,1,0:T(8,128)}, u32[]{:S(2)}) copy-start(f32[2,16,512]{2,1,0:T(8,128)} %param.8) | copy-start | bytes 196612
  82.0 43.0 %all-to-all-start.3 = ((f32[16,24,1024]{2,1,0:T(8,128)}), f32[16,24,1024]{2,1,0:T(8,128)S(1)}, u32[]{:S(2)}, u32[]{:S(2)}) async-start(f32[16,24,1024]{2,1,0:T(8,128)} %bitcast.75), calls=%async_computation.3 | async-start | bytes 3145728 | tf_op jit(solution)/shard_map/all_to_all | solution.py:48
  89.0 91.1 %all-gather.2.cloned.1.call-start = ((), (), s32[]{:S(2)}) async-start(), calls=%async_computation.9 | async-start | bytes 1081344 | tf_op jit(solution)/shard_map/all_gather | solution.py:101
  129.0 53.0 %all-to-all-start.4 = ((f32[16,512,32]{1,2,0:T(8,128)}), f32[16,512,32]{1,2,0:T(8,128)S(1)}, u32[]{:S(2)}, u32[]{:S(2)}) async-start(f32[16,512,32]{1,2,0:T(8,128)} %bitcast.19), calls=%async_computation.4 | async-start | bytes 2097152 | tf_op jit(solution)/shard_map/all_to_all | solution.py:48
  136.1 52.7 %copy-start.1 = (f32[2,24,512]{2,1,0:T(8,128)S(1)}, f32[2,24,512]{2,1,0:T(8,128)}, u32[]{:S(2)}) copy-start(f32[2,24,512]{2,1,0:T(8,128)} %param.6) | copy-start | bytes 294916
  183.0 15.6 %all-to-all-start.5 = ((f32[32,1,512]{2,1,0:T(1,128)}), f32[32,1,512]{2,1,0:T(1,128)S(1)}, u32[]{:S(2)}, u32[]{:S(2)}) async-start(f32[32,1,512]{2,1,0:T(1,128)} %reshape.94), calls=%async_computation.5 | async-start | bytes 131072 | tf_op jit(solution)/shard_map/all_to_all | solution.py:48
  200.8 15.8 %all-to-all-start.6 = ((f32[16,1,512]{2,1,0:T(1,128)}), f32[16,1,512]{2,1,0:T(1,128)S(1)}, u32[]{:S(2)}, u32[]{:S(2)}) async-start(f32[16,1,512]{2,1,0:T(1,128)} %reshape.96), calls=%async_computation.6 | async-start | bytes 65536 | tf_op jit(solution)/shard_map/all_to_all | solution.py:54
  220.6 28.1 %all-to-all-start.7 = ((f32[16,512,32]{1,2,0:T(8,128)}), f32[16,512,32]{1,2,0:T(8,128)S(1)}, u32[]{:S(2)}, u32[]{:S(2)}) async-start(f32[16,512,32]{1,2,0:T(8,128)} %bitcast.28), calls=%async_computation.7 | async-start | bytes 2097152 | tf_op jit(solution)/shard_map/all_to_all | solution.py:48
  249.7 18.7 %all-to-all-start.8 = ((f32[32,1,512]{2,1,0:T(1,128)}), f32[32,1,512]{2,1,0:T(1,128)S(1)}, u32[]{:S(2)}, u32[]{:S(2)}) async-start(f32[32,1,512]{2,1,0:T(1,128)} %reshape.98), calls=%async_computation.8 | async-start | bytes 131072 | tf_op jit(solution)/shard_map/all_to_all | solution.py:48
Sparse Core Ops, SparseCore 0:
  93.2 86.8 all-gather.1
